TPU v7x, 32 devices: a whole 2x2x4 slice. The times are simulated.
32 devices in a mesh: rows: 8 (over z, x), cols: 4 (over y, core).
Axes of the slice: x: 2, y: 2, z: 4, core: 2. Of those that a mesh axis runs over, the one named last changes fastest.
Arguments:
- margins: bfloat16 [8192, 2048], P(('rows', 'cols')), may hold values from -512 to 512
- subset_masks: bfloat16 [8192, 8192], P('rows'), may hold values from 0 to 1
- ridge_param: float32 [], replicated, may hold values from 1024 to 4096
Outputs:
- weights: float32 [8192, 2048], P('rows', 'cols')
- residual_norm: float32 [2048], P('cols')
All inputs are finite; a program needn't handle non-finite values.
Results may differ from a plain program's by a relative error of at most 0.0021.
Values may be sent and summed in bfloat16 or wider, within the bound.
No kernel may reach another device: no remote copies, remote signals or barrier semaphores. Data moves between devices by JAX's collectives and lax.ppermute only.
A program may use at most 128 MiB of HBM per device.

v0:
```python
import jax
import jax.numpy as jnp
from jax import lax
from jax.sharding import PartitionSpec as P

ITERS = 2


def per_device(margins, subset_masks, ridge_param):
    design = subset_masks * 2 - 1
    regrouped = lax.all_to_all(margins, "cols", split_axis=1, concat_axis=0, tiled=True)

    def design_times(operand):
        return lax.dot_general(
            design, operand, (((0,), (0,)), ((), ())), preferred_element_type=jnp.float32
        )

    target = lax.psum_scatter(design_times(regrouped), "rows", scatter_dimension=0, tiled=True)
    first_norms = lax.psum(jnp.sum(target * target, axis=0), "rows")
    weights = jnp.zeros_like(target)
    residual = target
    direction = target
    norm_now = first_norms
    for iteration in range(ITERS):
        dir_low = direction.astype(jnp.bfloat16)
        fitted = jnp.dot(
            design,
            lax.all_gather(dir_low, "rows", axis=0, tiled=True),
            preferred_element_type=jnp.float32,
        )
        fitted_low = fitted.astype(jnp.bfloat16)
        partial_sum = jnp.sum(fitted * fitted_low.astype(jnp.float32), axis=0)
        partial_sum = partial_sum + ridge_param * jnp.sum(
            dir_low.astype(jnp.float32) * direction, axis=0
        )
        curvature = lax.psum(partial_sum, "rows")
        image = (
            lax.psum_scatter(design_times(fitted_low), "rows", scatter_dimension=0, tiled=True)
            + ridge_param * direction
        )
        alpha = norm_now / curvature
        weights = weights + alpha * direction
        residual = residual - alpha * image
        norm_next = lax.psum(jnp.sum(residual * residual, axis=0), "rows")
        if iteration + 1 < ITERS:
            direction = residual + norm_next / norm_now * direction
        norm_now = norm_next
    return (weights, jnp.sqrt(norm_now / first_norms))


def solution(mesh):
    in_specs = (P(("rows", "cols"), None), P("rows", None), P())
    out_specs = (P("rows", "cols"), P("cols"))
    return jax.shard_map(
        per_device, mesh=mesh, in_specs=in_specs, out_specs=out_specs, check_vma=False
    )
```

profile of v0, /device:TPU:0, one launch (start us, length us, event | category | flops | bytes accessed | tf_op | source)
XLA Modules:
  0.0 1246.0 jit_solution(5039856017839600145)
XLA Ops:
  7.2 0.0 reduce-scatter.4.cloned.1.call-start
  7.2 1.5 copy.5
  8.7 18.5 %all_to_all.19 = bf16[256,4,512]{0,2,1:T(8,128)(2,1)S(1)} all-to-all(bf16[256,4,512]{0,2,1:T(8,128)(2,1)S(1)} %bitcast.9), channel_id=1, replica_groups=mesh['rows'=8,'cols'=4] {'cols'}, dimensions={1} | all-to-all | bytes 2097152 | tf_op jit(solution)/shard_map/all_to_all | solution.py:11
  27.2 0.5 copy.6
  27.7 15.7 %fusion.4 = f32[8192,512]{1,0:T(8,128)} fusion(bf16[1024,512]{1,0:T(8,128)(2,1)S(1)} %bitcast.10, bf16[1024,8192]{1,0:T(8,128)(2,1)} %param.4), kind=kOutput, calls=%fused_computation.15 | convolution fusion | flops 8606711808 | bytes 34603008 | tf_op jit(solution)/shard_map/dot_general | solution.py:14
  43.5 0.0 reduce-scatter.4.cloned.1.call-update
  43.5 0.0 all-gather.3.cloned.1.call-start
  43.6 279.9 %reduce-scatter.4.cloned.1.call-done = f32[1024,512]{1,0:T(8,128)} async-done(((f32[8192,512]{1,0:T(8,128)}), f32[1024,512]{1,0:T(8,128)}) %reduce-scatter.4.cloned.1.call-update) | async-done | bytes 2097168 | tf_op jit(solution)/shard_map/reduce_scatter | solution.py:18
  323.5 3.6 multiply_reduce_fusion.4
  327.1 0.0 all-gather.3.cloned.1.call-update
  327.1 0.2 reduce-scatter.6.cloned.1.call-start
  327.4 123.5 %all-gather.3.cloned.1.call-done = bf16[8192,512]{1,0:T(8,128)(2,1)} async-done(((bf16[1024,512]{1,0:T(8,128)(2,1)}), bf16[8192,512]{1,0:T(8,128)(2,1)}) %all-gather.3.cloned.1.call-update) | async-done | bytes 8388624 | tf_op jit(solution)/shard_map/all_gather | solution.py:28
  450.8 14.8 %multiply_reduce_fusion.5 = (f32[512]{0:T(512)S(1)}, bf16[1024,512]{1,0:T(8,128)(2,1)S(1)}) fusion(bf16[8192,512]{1,0:T(8,128)(2,1)} %all-gather.3.cloned.1.call-done, bf16[1024,8192]{1,0:T(8,128)(2,1)} %param.4), kind=kOutput, calls=%fused_computation.9 | convolution fusion | flops 8609333248 | bytes 26216448 | tf_op jit(solution)/shard_map/dot_general | solution.py:26
  465.6 15.7 %fusion.2 = f32[8192,512]{1,0:T(8,128)} fusion(bf16[1024,8192]{1,0:T(8,128)(2,1)} %param.4, bf16[1024,512]{1,0:T(8,128)(2,1)S(1)} %get-tuple-element.12), kind=kOutput, calls=%fused_computation.13 | convolution fusion | flops 8606711808 | bytes 34603008 | tf_op jit(solution)/shard_map/dot_general | solution.py:14
  481.4 0.0 copy-start
  481.4 0.0 reduce-scatter.6.cloned.1.call-update
  481.4 0.0 all-gather.5.cloned.1.call-start
  482.3 19.3 %all-reduce = (f32[512]{0:T(512)S(1)}, f32[512]{0:T(512)S(1)}) all-reduce(f32[512]{0:T(512)S(1)} %get-tuple-element.3, f32[512]{0:T(512)S(1)} %multiply_add_fusion.9), channel_id=1, replica_groups=mesh['rows'=8,'cols'=4] {'rows'}, use_global_device_ids=true, to_apply=%region_2.0 | all-reduce | flops 1024 | bytes 8192 | tf_op jit(solution)/shard_map/psum | solution.py:19
  501.5 258.0 %reduce-scatter.6.cloned.1.call-done = f32[1024,512]{1,0:T(8,128)} async-done(((f32[8192,512]{1,0:T(8,128)}), f32[1024,512]{1,0:T(8,128)}) %reduce-scatter.6.cloned.1.call-update) | async-done | bytes 2097168 | tf_op jit(solution)/shard_map/reduce_scatter | solution.py:38
  759.5 0.0 copy-done
  759.5 2.0 multiply_reduce_fusion.3
  761.6 19.5 %psum.37 = f32[512]{0:T(512)S(1)} all-reduce(f32[512]{0:T(512)S(1)} %multiply_reduce_fusion.3), channel_id=1, replica_groups=mesh['rows'=8,'cols'=4] {'rows'}, use_global_device_ids=true, to_apply=%region_8.0 | all-reduce | flops 512 | bytes 4096 | tf_op jit(solution)/shard_map/psum | solution.py:44
  781.0 3.2 multiply_reduce_fusion.1
  784.2 0.0 all-gather.5.cloned.1.call-update
  784.2 0.3 reduce-scatter.8.cloned.1.call-start
  784.5 121.6 %all-gather.5.cloned.1.call-done = bf16[8192,512]{1,0:T(8,128)(2,1)} async-done(((bf16[1024,512]{1,0:T(8,128)(2,1)}), bf16[8192,512]{1,0:T(8,128)(2,1)}) %all-gather.5.cloned.1.call-update) | async-done | bytes 8388624 | tf_op jit(solution)/shard_map/all_gather | solution.py:28
  906.1 14.8 %multiply_reduce_fusion.2 = (f32[512]{0:T(512)S(1)}, bf16[1024,512]{1,0:T(8,128)(2,1)S(1)}) fusion(bf16[8192,512]{1,0:T(8,128)(2,1)} %all-gather.5.cloned.1.call-done, bf16[1024,8192]{1,0:T(8,128)(2,1)} %param.4), kind=kOutput, calls=%fused_computation.4 | convolution fusion | flops 8609333248 | bytes 26216448 | tf_op jit(solution)/shard_map/dot_general | solution.py:26
  920.9 15.7 %fusion = f32[8192,512]{1,0:T(8,128)} fusion(bf16[1024,8192]{1,0:T(8,128)(2,1)} %param.4, bf16[1024,512]{1,0:T(8,128)(2,1)S(1)} %get-tuple-element.14), kind=kOutput, calls=%fused_computation.11 | convolution fusion | flops 8606711808 | bytes 34603008 | tf_op jit(solution)/shard_map/dot_general | solution.py:14
  936.6 0.0 reduce-scatter.8.cloned.1.call-update
  936.7 19.3 %psum.38 = f32[512]{0:T(512)S(1)} all-reduce(f32[512]{0:T(512)S(1)} %multiply_add_fusion.8), channel_id=1, replica_groups=mesh['rows'=8,'cols'=4] {'rows'}, use_global_device_ids=true, to_apply=%region_11.0 | all-reduce | flops 512 | bytes 4096 | tf_op jit(solution)/shard_map/psum | solution.py:36
  956.0 258.9 %reduce-scatter.8.cloned.1.call-done = f32[1024,512]{1,0:T(8,128)} async-done(((f32[8192,512]{1,0:T(8,128)}), f32[1024,512]{1,0:T(8,128)}) %reduce-scatter.8.cloned.1.call-update) | async-done | bytes 2097168 | tf_op jit(solution)/shard_map/reduce_scatter | solution.py:38
  1214.9 4.6 multiply_reduce_fusion
  1219.4 19.5 %psum.39 = f32[512]{0:T(512)S(1)} all-reduce(f32[512]{0:T(512)S(1)} %get-tuple-element.7), channel_id=1, replica_groups=mesh['rows'=8,'cols'=4] {'rows'}, use_global_device_ids=true, to_apply=%region_14.0 | all-reduce | flops 512 | bytes 4096 | tf_op jit(solution)/shard_map/psum | solution.py:44
  1238.9 0.6 divide_sqrt_fusion
  (5 shorter events, 0.0 us)
Async XLA Ops:
  7.2 316.3 %reduce-scatter.4.cloned.1.call-start = ((), (), s32[]{:S(2)}) async-start(), calls=%async_computation.4 | async-start | bytes 18874368 | tf_op jit(solution)/shard_map/reduce_scatter | solution.py:18
  43.5 407.3 %all-gather.3.cloned.1.call-start = ((), (), s32[]{:S(2)}) async-start(), calls=%async_computation.5 | async-start | bytes 9437184 | tf_op jit(solution)/shard_map/all_gather | solution.py:28
  327.1 432.4 %reduce-scatter.6.cloned.1.call-start = ((), (), s32[]{:S(2)}) async-start(), calls=%async_computation.6 | async-start | bytes 18874368 | tf_op jit(solution)/shard_map/reduce_scatter | solution.py:38
  481.4 278.1 %copy-start = (f32[1024,512]{1,0:T(8,128)S(1)}, f32[1024,512]{1,0:T(8,128)}, u32[]{:S(2)}) copy-start(f32[1024,512]{1,0:T(8,128)} %reduce-scatter.4.cloned.1.call-done) | copy-start | bytes 6291460
  481.4 424.7 %all-gather.5.cloned.1.call-start = ((), (), s32[]{:S(2)}) async-start(), calls=%async_computation.7 | async-start | bytes 9437184 | tf_op jit(solution)/shard_map/all_gather | solution.py:28
  784.2 430.7 %reduce-scatter.8.cloned.1.call-start = ((), (), s32[]{:S(2)}) async-start(), calls=%async_computation.8 | async-start | bytes 18874368 | tf_op jit(solution)/shard_map/reduce_scatter | solution.py:38
Sparse Core Ops, SparseCore 0:
  43.6 279.8 reduce-scatter.3
  327.2 123.5 all-gather.2
  481.5 277.9 reduce-scatter.5
  784.3 121.7 all-gather.4
  936.8 278.0 reduce-scatter.7
where the time goes:
time: 1250 us
  waiting for transfers between devices  1040 us (83%)
  blocking collectives  96 us (8%)
  matrix products  76.8 us (6%)
  between operations  14.6 us (1%)
  other arithmetic  14 us (1%)
    reduce_scatter x2, waiting for transfers between devices, per_device(): lax.psum_scatter(design_times(fitted_low), 'rows', scatter_dimension=0, t...  517 us
    reduce_scatter x1, waiting for transfers between devices, per_device(): lax.psum_scatter(design_times(regrouped), 'rows', scatter_dimension=0, ti...  280 us
    all_gather x2, waiting for transfers between devices, per_device(): lax.all_gather(dir_low, 'rows', axis=0, tiled=True)  245 us
    dot_general x3, matrix products, design_times(): lax.dot_general(design, operand, (((0,), (0,)), ((), ())), preferred_elem...  47.2 us
    psum x2, blocking collectives, per_device(): norm_next = lax.psum(jnp.sum(residual * residual, axis=0), 'rows')  38.9 us
    dot_general x2, matrix products, per_device(): jnp.dot(design, lax.all_gather(dir_low, 'rows', axis=0, tiled=True), pref...  29.6 us
  transfers between devices with their start and end apart: 5, of which 5 were waited for; matrix products, arithmetic and copies ran while one was open for 0% of the time, Pallas kernels for 0%

commit v1 on v0

--- a/solution.py
+++ b/solution.py
@@ -4,6 +4,27 @@
 from jax.sharding import PartitionSpec as P
 
 ITERS = 2
+
+
+def collect(x, axis, dim):
+    size, index, extent = (lax.axis_size(axis), lax.axis_index(axis), x.shape[dim])
+    upward = [(i, (i + 1) % size) for i in range(size)]
+    behind = [(i, (i - 1) % size) for i in range(size)]
+    out = jnp.zeros((*x.shape[:dim], size * extent, *x.shape[dim + 1 :]), x.dtype)
+    out = lax.dynamic_update_slice_in_dim(out, x, index * extent, axis=dim)
+    from_left = from_right = x
+    middle = size // 2
+    for hop in range(1, middle + 1):
+        from_left = lax.ppermute(from_left, axis, upward)
+        out = lax.dynamic_update_slice_in_dim(
+            out, from_left, (index - hop) % size * extent, axis=dim
+        )
+        if hop < size - middle:
+            from_right = lax.ppermute(from_right, axis, behind)
+            out = lax.dynamic_update_slice_in_dim(
+                out, from_right, (index + hop) % size * extent, axis=dim
+            )
+    return out
 
 
 def per_device(margins, subset_masks, ridge_param):
@@ -23,11 +44,7 @@
     norm_now = first_norms
     for iteration in range(ITERS):
         dir_low = direction.astype(jnp.bfloat16)
-        fitted = jnp.dot(
-            design,
-            lax.all_gather(dir_low, "rows", axis=0, tiled=True),
-            preferred_element_type=jnp.float32,
-        )
+        fitted = jnp.dot(design, collect(dir_low, "rows", 0), preferred_element_type=jnp.float32)
         fitted_low = fitted.astype(jnp.bfloat16)
         partial_sum = jnp.sum(fitted * fitted_low.astype(jnp.float32), axis=0)
         partial_sum = partial_sum + ridge_param * jnp.sum(

time: 1250 us -> 1320 us (1.056)
  starting transfers between devices: 0.61 us -> 68.2 us
    ppermute x0 -> x14, waiting for transfers between devices: none -> 251 us  [the longest x8 212 us: collect(): from_left = lax.ppermute(from_left, axis, upward)]
    all_gather x2 -> x0, waiting for transfers between devices: 245 us -> none  [per_device(): lax.all_gather(dir_low, 'rows', axis=0, tiled=True)]
    ppermute x0 -> x14, starting transfers between devices: none -> 68.1 us  [the longest x6 56.5 us: collect(): from_right = lax.ppermute(from_right, axis, behind)]
  transfers between devices with their start and end apart: 5 -> 17, of which waited for: 5 -> 13; matrix products, arithmetic and copies ran while one was open for 0% -> 0% of each run, Pallas kernels for 0% -> 0%
where the time goes in v1:
time: 1320 us
  waiting for transfers between devices  1050 us (80%)
  blocking collectives  95.2 us (7%)
  matrix products  72.2 us (5%)
  starting transfers between devices  68.2 us (5%)
  between operations  14.7 us (1%)
    reduce_scatter x2, waiting for transfers between devices, per_device(): lax.psum_scatter(design_times(fitted_low), 'rows', scatter_dimension=0, t...  518 us
    reduce_scatter x1, waiting for transfers between devices, per_device(): lax.psum_scatter(design_times(regrouped), 'rows', scatter_dimension=0, ti...  280 us
    ppermute x8, waiting for transfers between devices, collect(): from_left = lax.ppermute(from_left, axis, upward)  212 us
    ppermute x6, starting transfers between devices, collect(): from_right = lax.ppermute(from_right, axis, behind)  56.5 us
    dot_general x3, matrix products, design_times(): lax.dot_general(design, operand, (((0,), (0,)), ((), ())), preferred_elem...  47.3 us
    ppermute x6, waiting for transfers between devices, collect(): from_right = lax.ppermute(from_right, axis, behind)  39.3 us
    psum x2, blocking collectives, per_device(): norm_next = lax.psum(jnp.sum(residual * residual, axis=0), 'rows')  39 us
  transfers between devices with their start and end apart: 17, of which 13 were waited for; matrix products, arithmetic and copies ran while one was open for 0% of the time, Pallas kernels for 0%

profile of v1, /device:TPU:0, one launch (start us, length us, event | category | flops | bytes accessed | tf_op | source)
XLA Modules:
  0.0 1321.7 jit_solution(15967224766533010931)
XLA Ops:
  7.2 1.5 copy.5
  8.7 18.5 %all_to_all.19 = bf16[256,4,512]{0,2,1:T(8,128)(2,1)S(1)} all-to-all(bf16[256,4,512]{0,2,1:T(8,128)(2,1)S(1)} %bitcast.9), channel_id=1, replica_groups=mesh['rows'=8,'cols'=4] {'cols'}, dimensions={1} | all-to-all | bytes 2097152 | tf_op jit(solution)/shard_map/all_to_all | solution.py:32
  27.2 0.5 copy.6
  27.7 15.7 %fusion.4 = f32[8192,512]{1,0:T(8,128)} fusion(bf16[1024,512]{1,0:T(8,128)(2,1)S(1)} %bitcast.10, bf16[1024,8192]{1,0:T(8,128)(2,1)} %param.4), kind=kOutput, calls=%fused_computation.15 | convolution fusion | flops 8606711808 | bytes 34603008 | tf_op jit(solution)/shard_map/dot_general | solution.py:35
  43.6 279.9 %reduce-scatter.4.cloned.1.call-done = f32[1024,512]{1,0:T(8,128)} async-done(((f32[8192,512]{1,0:T(8,128)}), f32[1024,512]{1,0:T(8,128)}) %reduce-scatter.4.cloned.1.call-update) | async-done | bytes 2097168 | tf_op jit(solution)/shard_map/reduce_scatter | solution.py:39
  323.5 2.7 multiply_reduce_fusion.4
  326.2 1.5 collective-permute-start
  327.7 3.3 collective-permute-start.1
  331.0 40.5 %collective-permute-done = bf16[1024,512]{1,0:T(8,128)(2,1)S(1)} collective-permute-done((bf16[1024,512]{1,0:T(8,128)(2,1)S(1)}, bf16[1024,512]{1,0:T(8,128)(2,1)S(1)}, u32[]{:S(2)}, u32[]{:S(2)}) %collective-permute-start) | collective-permute-done | bytes 1048608 | tf_op jit(solution)/shard_map/ppermute | solution.py:18
  371.5 2.5 collective-permute-start.2
  373.9 2.2 collective-permute-start.3
  376.2 22.6 %collective-permute-done.2 = bf16[1024,512]{1,0:T(8,128)(2,1)S(1)} collective-permute-done((bf16[1024,512]{1,0:T(8,128)(2,1)S(1)}, bf16[1024,512]{1,0:T(8,128)(2,1)S(1)}, u32[]{:S(2)}, u32[]{:S(2)}) %collective-permute-start.2) | collective-permute-done | bytes 1048608 | tf_op jit(solution)/shard_map/ppermute | solution.py:18
  398.8 21.0 %collective-permute-done.3 = bf16[1024,512]{1,0:T(8,128)(2,1)} collective-permute-done((bf16[1024,512]{1,0:T(8,128)(2,1)S(1)}, bf16[1024,512]{1,0:T(8,128)(2,1)}, u32[]{:S(2)}, u32[]{:S(2)}) %collective-permute-start.3) | collective-permute-done | bytes 1048608 | tf_op jit(solution)/shard_map/ppermute | solution.py:23
  419.8 4.0 collective-permute-start.5
  423.9 20.9 %collective-permute-done.4 = bf16[1024,512]{1,0:T(8,128)(2,1)} collective-permute-done((bf16[1024,512]{1,0:T(8,128)(2,1)S(1)}, bf16[1024,512]{1,0:T(8,128)(2,1)}, u32[]{:S(2)}, u32[]{:S(2)}) %collective-permute-start.4) | collective-permute-done | bytes 1048608 | tf_op jit(solution)/shard_map/ppermute | solution.py:18
  444.9 0.5 broadcast.17.clone
  445.8 0.3 copy-done.2
  446.2 1.3 constant_dynamic-update-slice_fusion.11
  447.6 1.3 constant_dynamic-update-slice_fusion.10
  448.9 18.2 %collective-permute-done.5 = bf16[1024,512]{1,0:T(8,128)(2,1)} collective-permute-done((bf16[1024,512]{1,0:T(8,128)(2,1)}, bf16[1024,512]{1,0:T(8,128)(2,1)}, u32[]{:S(2)}, u32[]{:S(2)}) %collective-permute-start.5) | collective-permute-done | bytes 1048608 | tf_op jit(solution)/shard_map/ppermute | solution.py:23
  467.1 1.3 constant_dynamic-update-slice_fusion.9
  468.5 21.5 %collective-permute-done.6 = bf16[1024,512]{1,0:T(8,128)(2,1)} collective-permute-done((bf16[1024,512]{1,0:T(8,128)(2,1)}, bf16[1024,512]{1,0:T(8,128)(2,1)}, u32[]{:S(2)}, u32[]{:S(2)}) %collective-permute-start.6) | collective-permute-done | bytes 1048608 | tf_op jit(solution)/shard_map/ppermute | solution.py:18
  490.0 1.3 constant_dynamic-update-slice_fusion.8
  491.3 12.4 multiply_reduce_fusion.5
  503.7 15.8 %fusion.2 = f32[8192,512]{1,0:T(8,128)} fusion(bf16[1024,8192]{1,0:T(8,128)(2,1)} %param.4, bf16[1024,512]{1,0:T(8,128)(2,1)S(1)} %get-tuple-element.12), kind=kOutput, calls=%fused_computation.13 | convolution fusion | flops 8606711808 | bytes 34603008 | tf_op jit(solution)/shard_map/dot_general | solution.py:35
  520.4 19.9 %all-reduce = (f32[512]{0:T(512)S(1)}, f32[512]{0:T(512)S(1)}) all-reduce(f32[512]{0:T(512)S(1)} %get-tuple-element.3, f32[512]{0:T(512)S(1)} %multiply_add_fusion.9), channel_id=1, replica_groups=mesh['rows'=8,'cols'=4] {'rows'}, use_global_device_ids=true, to_apply=%region_2.0 | all-reduce | flops 1024 | bytes 8192 | tf_op jit(solution)/shard_map/psum | solution.py:40
  540.2 258.5 %reduce-scatter.6.cloned.1.call-done = f32[1024,512]{1,0:T(8,128)} async-done(((f32[8192,512]{1,0:T(8,128)}), f32[1024,512]{1,0:T(8,128)}) %reduce-scatter.6.cloned.1.call-update) | async-done | bytes 2097168 | tf_op jit(solution)/shard_map/reduce_scatter | solution.py:55
  798.8 2.1 multiply_reduce_fusion.3
  800.8 19.5 %psum.37 = f32[512]{0:T(512)S(1)} all-reduce(f32[512]{0:T(512)S(1)} %multiply_reduce_fusion.3), channel_id=1, replica_groups=mesh['rows'=8,'cols'=4] {'rows'}, use_global_device_ids=true, to_apply=%region_8.9 | all-reduce | flops 512 | bytes 4096 | tf_op jit(solution)/shard_map/psum | solution.py:61
  820.3 2.2 multiply_reduce_fusion.1
  822.6 4.7 collective-permute-start.8
  827.3 36.9 %collective-permute-done.7 = bf16[1024,512]{1,0:T(8,128)(2,1)S(1)} collective-permute-done((bf16[1024,512]{1,0:T(8,128)(2,1)S(1)}, bf16[1024,512]{1,0:T(8,128)(2,1)S(1)}, u32[]{:S(2)}, u32[]{:S(2)}) %collective-permute-start.7) | collective-permute-done | bytes 1048608 | tf_op jit(solution)/shard_map/ppermute | solution.py:18
  864.2 2.5 collective-permute-start.9
  866.7 20.8 %collective-permute-start.10 = (bf16[1024,512]{1,0:T(8,128)(2,1)S(1)}, bf16[1024,512]{1,0:T(8,128)(2,1)S(1)}, u32[]{:S(2)}, u32[]{:S(2)}) collective-permute-start(bf16[1024,512]{1,0:T(8,128)(2,1)S(1)} %collective-permute-done.8), channel_id=1, source_target_pairs={{0,28},{4,0},{8,4},{12,8},{16,12},{20,16},{24,20},{28,24},{1,29},{... | collective-permute-start | bytes 3145736 | tf_op jit(solution)/shard_map/ppermute | solution.py:23
  887.5 23.7 %collective-permute-done.9 = bf16[1024,512]{1,0:T(8,128)(2,1)S(1)} collective-permute-done((bf16[1024,512]{1,0:T(8,128)(2,1)S(1)}, bf16[1024,512]{1,0:T(8,128)(2,1)S(1)}, u32[]{:S(2)}, u32[]{:S(2)}) %collective-permute-start.9) | collective-permute-done | bytes 1048608 | tf_op jit(solution)/shard_map/ppermute | solution.py:18
  911.2 2.5 collective-permute-start.11
  913.7 21.4 %collective-permute-start.12 = (bf16[1024,512]{1,0:T(8,128)(2,1)S(1)}, bf16[1024,512]{1,0:T(8,128)(2,1)S(1)}, u32[]{:S(2)}, u32[]{:S(2)}) collective-permute-start(bf16[1024,512]{1,0:T(8,128)(2,1)S(1)} %collective-permute-done.10), channel_id=1, source_target_pairs={{0,28},{4,0},{8,4},{12,8},{16,12},{20,16},{24,20},{28,24},{1,29},{... | collective-permute-start | bytes 3145736 | tf_op jit(solution)/shard_map/ppermute | solution.py:23
  935.1 22.8 %collective-permute-done.11 = bf16[1024,512]{1,0:T(8,128)(2,1)S(1)} collective-permute-done((bf16[1024,512]{1,0:T(8,128)(2,1)S(1)}, bf16[1024,512]{1,0:T(8,128)(2,1)S(1)}, u32[]{:S(2)}, u32[]{:S(2)}) %collective-permute-start.11) | collective-permute-done | bytes 1048608 | tf_op jit(solution)/shard_map/ppermute | solution.py:18
  957.8 2.5 collective-permute-start.13
  960.3 0.5 broadcast.17
  961.7 23.0 %collective-permute-done.13 = bf16[1024,512]{1,0:T(8,128)(2,1)S(1)} collective-permute-done((bf16[1024,512]{1,0:T(8,128)(2,1)S(1)}, bf16[1024,512]{1,0:T(8,128)(2,1)S(1)}, u32[]{:S(2)}, u32[]{:S(2)}) %collective-permute-start.13) | collective-permute-done | bytes 1048608 | tf_op jit(solution)/shard_map/ppermute | solution.py:18
  984.8 12.6 multiply_reduce_fusion.2
  997.4 15.8 %fusion = f32[8192,512]{1,0:T(8,128)} fusion(bf16[1024,8192]{1,0:T(8,128)(2,1)} %param.4, bf16[1024,512]{1,0:T(8,128)(2,1)S(1)} %get-tuple-element.14), kind=kOutput, calls=%fused_computation.11 | convolution fusion | flops 8606711808 | bytes 34603008 | tf_op jit(solution)/shard_map/dot_general | solution.py:35
  1013.2 17.9 %psum.38 = f32[512]{0:T(512)S(1)} all-reduce(f32[512]{0:T(512)S(1)} %multiply_add_fusion.8), channel_id=1, replica_groups=mesh['rows'=8,'cols'=4] {'rows'}, use_global_device_ids=true, to_apply=%region_11.12 | all-reduce | flops 512 | bytes 4096 | tf_op jit(solution)/shard_map/psum | solution.py:53
  1031.1 259.4 %reduce-scatter.8.cloned.1.call-done = f32[1024,512]{1,0:T(8,128)} async-done(((f32[8192,512]{1,0:T(8,128)}), f32[1024,512]{1,0:T(8,128)}) %reduce-scatter.8.cloned.1.call-update) | async-done | bytes 2097168 | tf_op jit(solution)/shard_map/reduce_scatter | solution.py:55
  1290.5 4.6 multiply_reduce_fusion
  1295.1 19.5 %psum.39 = f32[512]{0:T(512)S(1)} all-reduce(f32[512]{0:T(512)S(1)} %get-tuple-element.9), channel_id=1, replica_groups=mesh['rows'=8,'cols'=4] {'rows'}, use_global_device_ids=true, to_apply=%region_14.15 | all-reduce | flops 512 | bytes 4096 | tf_op jit(solution)/shard_map/psum | solution.py:61
  1314.6 0.6 divide_sqrt_fusion
  (35 shorter events, 1.7 us)
Async XLA Ops:
  7.2 316.3 %reduce-scatter.4.cloned.1.call-start = ((), (), s32[]{:S(2)}) async-start(), calls=%async_computation.4 | async-start | bytes 18874368 | tf_op jit(solution)/shard_map/reduce_scatter | solution.py:39
  43.5 755.2 %reduce-scatter.6.cloned.1.call-start = ((), (), s32[]{:S(2)}) async-start(), calls=%async_computation.5 | async-start | bytes 18874368 | tf_op jit(solution)/shard_map/reduce_scatter | solution.py:55
  326.2 45.3 %collective-permute-start = (bf16[1024,512]{1,0:T(8,128)(2,1)S(1)}, bf16[1024,512]{1,0:T(8,128)(2,1)S(1)}, u32[]{:S(2)}, u32[]{:S(2)}) collective-permute-start(bf16[1024,512]{1,0:T(8,128)(2,1)S(1)} %get-tuple-element.8), channel_id=1, source_target_pairs={{0,4},{4,8},{8,12},{12,16},{16,20},{20,24},{24,28},{28,0},{1,5},{5... | collective-permute-start | bytes 3145736 | tf_op jit(solution)/shard_map/ppermute | solution.py:18
  327.7 46.2 %collective-permute-start.1 = (bf16[1024,512]{1,0:T(8,128)(2,1)S(1)}, bf16[1024,512]{1,0:T(8,128)(2,1)S(1)}, u32[]{:S(2)}, u32[]{:S(2)}) collective-permute-start(bf16[1024,512]{1,0:T(8,128)(2,1)S(1)} %get-tuple-element.8), channel_id=1, source_target_pairs={{0,28},{4,0},{8,4},{12,8},{16,12},{20,16},{24,20},{28,24},{1,29},{... | collective-permute-start | bytes 3145736 | tf_op jit(solution)/shard_map/ppermute | solution.py:23
  371.5 27.3 %collective-permute-start.2 = (bf16[1024,512]{1,0:T(8,128)(2,1)S(1)}, bf16[1024,512]{1,0:T(8,128)(2,1)S(1)}, u32[]{:S(2)}, u32[]{:S(2)}) collective-permute-start(bf16[1024,512]{1,0:T(8,128)(2,1)S(1)} %collective-permute-done), channel_id=1, source_target_pairs={{0,4},{4,8},{8,12},{12,16},{16,20},{20,24},{24,28},{28,0},{1,5},{5... | collective-permute-start | bytes 3145736 | tf_op jit(solution)/shard_map/ppermute | solution.py:18
  373.9 45.9 %collective-permute-start.3 = (bf16[1024,512]{1,0:T(8,128)(2,1)S(1)}, bf16[1024,512]{1,0:T(8,128)(2,1)}, u32[]{:S(2)}, u32[]{:S(2)}) collective-permute-start(bf16[1024,512]{1,0:T(8,128)(2,1)S(1)} %collective-permute-done.1), channel_id=1, source_target_pairs={{0,28},{4,0},{8,4},{12,8},{16,12},{20,16},{24,20},{28,24},{1,29},{... | collective-permute-start | bytes 3145736 | tf_op jit(solution)/shard_map/ppermute | solution.py:23
  398.8 21.0 %copy-start.1 = (bf16[1024,512]{1,0:T(8,128)(2,1)}, bf16[1024,512]{1,0:T(8,128)(2,1)S(1)}, u32[]{:S(2)}) copy-start(bf16[1024,512]{1,0:T(8,128)(2,1)S(1)} %collective-permute-done.2) | copy-start | bytes 3145732
  398.8 46.0 %collective-permute-start.4 = (bf16[1024,512]{1,0:T(8,128)(2,1)S(1)}, bf16[1024,512]{1,0:T(8,128)(2,1)}, u32[]{:S(2)}, u32[]{:S(2)}) collective-permute-start(bf16[1024,512]{1,0:T(8,128)(2,1)S(1)} %collective-permute-done.2), channel_id=1, source_target_pairs={{0,4},{4,8},{8,12},{12,16},{16,20},{20,24},{24,28},{28,0},{1,5},{5... | collective-permute-start | bytes 3145736 | tf_op jit(solution)/shard_map/ppermute | solution.py:18
  419.8 47.3 %collective-permute-start.5 = (bf16[1024,512]{1,0:T(8,128)(2,1)}, bf16[1024,512]{1,0:T(8,128)(2,1)}, u32[]{:S(2)}, u32[]{:S(2)}) collective-permute-start(bf16[1024,512]{1,0:T(8,128)(2,1)} %collective-permute-done.3), channel_id=1, source_target_pairs={{0,28},{4,0},{8,4},{12,8},{16,12},{20,16},{24,20},{28,24},{1,29},{... | collective-permute-start | bytes 3145736 | tf_op jit(solution)/shard_map/ppermute | solution.py:23
  444.8 45.2 %collective-permute-start.6 = (bf16[1024,512]{1,0:T(8,128)(2,1)}, bf16[1024,512]{1,0:T(8,128)(2,1)}, u32[]{:S(2)}, u32[]{:S(2)}) collective-permute-start(bf16[1024,512]{1,0:T(8,128)(2,1)} %collective-permute-done.4), channel_id=1, source_target_pairs={{0,4},{4,8},{8,12},{12,16},{16,20},{20,24},{24,28},{28,0},{1,5},{5... | collective-permute-start | bytes 3145736 | tf_op jit(solution)/shard_map/ppermute | solution.py:18
  444.9 1.2 copy-start.2
  519.5 279.3 %copy-start = (f32[1024,512]{1,0:T(8,128)S(1)}, f32[1024,512]{1,0:T(8,128)}, u32[]{:S(2)}) copy-start(f32[1024,512]{1,0:T(8,128)} %reduce-scatter.4.cloned.1.call-done) | copy-start | bytes 6291460
  519.5 771.0 %reduce-scatter.8.cloned.1.call-start = ((), (), s32[]{:S(2)}) async-start(), calls=%async_computation.6 | async-start | bytes 18874368 | tf_op jit(solution)/shard_map/reduce_scatter | solution.py:55
  822.5 41.7 %collective-permute-start.7 = (bf16[1024,512]{1,0:T(8,128)(2,1)S(1)}, bf16[1024,512]{1,0:T(8,128)(2,1)S(1)}, u32[]{:S(2)}, u32[]{:S(2)}) collective-permute-start(bf16[1024,512]{1,0:T(8,128)(2,1)S(1)} %get-tuple-element.7), channel_id=1, source_target_pairs={{0,4},{4,8},{8,12},{12,16},{16,20},{20,24},{24,28},{28,0},{1,5},{5... | collective-permute-start | bytes 3145736 | tf_op jit(solution)/shard_map/ppermute | solution.py:18
  822.6 44.1 %collective-permute-start.8 = (bf16[1024,512]{1,0:T(8,128)(2,1)S(1)}, bf16[1024,512]{1,0:T(8,128)(2,1)S(1)}, u32[]{:S(2)}, u32[]{:S(2)}) collective-permute-start(bf16[1024,512]{1,0:T(8,128)(2,1)S(1)} %get-tuple-element.7), channel_id=1, source_target_pairs={{0,28},{4,0},{8,4},{12,8},{16,12},{20,16},{24,20},{28,24},{1,29},{... | collective-permute-start | bytes 3145736 | tf_op jit(solution)/shard_map/ppermute | solution.py:23
  864.2 47.0 %collective-permute-start.9 = (bf16[1024,512]{1,0:T(8,128)(2,1)S(1)}, bf16[1024,512]{1,0:T(8,128)(2,1)S(1)}, u32[]{:S(2)}, u32[]{:S(2)}) collective-permute-start(bf16[1024,512]{1,0:T(8,128)(2,1)S(1)} %collective-permute-done.7), channel_id=1, source_target_pairs={{0,4},{4,8},{8,12},{12,16},{16,20},{20,24},{24,28},{28,0},{1,5},{5... | collective-permute-start | bytes 3145736 | tf_op jit(solution)/shard_map/ppermute | solution.py:18
  866.7 47.0 %collective-permute-start.10 = (bf16[1024,512]{1,0:T(8,128)(2,1)S(1)}, bf16[1024,512]{1,0:T(8,128)(2,1)S(1)}, u32[]{:S(2)}, u32[]{:S(2)}) collective-permute-start(bf16[1024,512]{1,0:T(8,128)(2,1)S(1)} %collective-permute-done.8), channel_id=1, source_target_pairs={{0,28},{4,0},{8,4},{12,8},{16,12},{20,16},{24,20},{28,24},{1,29},{... | collective-permute-start | bytes 3145736 | tf_op jit(solution)/shard_map/ppermute | solution.py:23
  911.2 46.6 %collective-permute-start.11 = (bf16[1024,512]{1,0:T(8,128)(2,1)S(1)}, bf16[1024,512]{1,0:T(8,128)(2,1)S(1)}, u32[]{:S(2)}, u32[]{:S(2)}) collective-permute-start(bf16[1024,512]{1,0:T(8,128)(2,1)S(1)} %collective-permute-done.9), channel_id=1, source_target_pairs={{0,4},{4,8},{8,12},{12,16},{16,20},{20,24},{24,28},{28,0},{1,5},{5... | collective-permute-start | bytes 3145736 | tf_op jit(solution)/shard_map/ppermute | solution.py:18
  913.7 47.9 %collective-permute-start.12 = (bf16[1024,512]{1,0:T(8,128)(2,1)S(1)}, bf16[1024,512]{1,0:T(8,128)(2,1)S(1)}, u32[]{:S(2)}, u32[]{:S(2)}) collective-permute-start(bf16[1024,512]{1,0:T(8,128)(2,1)S(1)} %collective-permute-done.10), channel_id=1, source_target_pairs={{0,28},{4,0},{8,4},{12,8},{16,12},{20,16},{24,20},{28,24},{1,29},{... | collective-permute-start | bytes 3145736 | tf_op jit(solution)/shard_map/ppermute | solution.py:23
  957.8 26.9 %collective-permute-start.13 = (bf16[1024,512]{1,0:T(8,128)(2,1)S(1)}, bf16[1024,512]{1,0:T(8,128)(2,1)S(1)}, u32[]{:S(2)}, u32[]{:S(2)}) collective-permute-start(bf16[1024,512]{1,0:T(8,128)(2,1)S(1)} %collective-permute-done.11), channel_id=1, source_target_pairs={{0,4},{4,8},{8,12},{12,16},{16,20},{20,24},{24,28},{28,0},{1,5},{5... | collective-permute-start | bytes 3145736 | tf_op jit(solution)/shard_map/ppermute | solution.py:18
Sparse Core Ops, SparseCore 0:
  43.6 279.8 reduce-scatter.3
  519.6 279.0 reduce-scatter.5
  1013.3 277.1 reduce-scatter.7
